TPU v7x, 512 devices: a whole 4x8x8 slice. The times are simulated.
512 devices in a mesh: cfg: 2 (over x_lo), ctx: 32 (over y, x_hi, core), tp: 8 (over z).
Axes of the slice: x: 4 (x_hi: 2, x_lo: 2; x = x_hi * 2 + x_lo), y: 8, z: 8, core: 2. Of those that a mesh axis runs over, the one named last changes fastest.
Arguments:
- query_proj: bfloat16 [2, 8192, 3072], P('cfg', 'ctx', 'tp'), may hold values from -8 to 8
- key_proj: bfloat16 [2, 8192, 3072], P('cfg', 'ctx', 'tp'), may hold values from -8 to 8
- value_proj: bfloat16 [2, 8192, 3072], P('cfg', 'ctx', 'tp'), may hold values from -6 to 6
- query_gain: float32 [128], replicated, may hold values from 1 to 8
- key_gain: float32 [128], replicated, may hold values from 1 to 8
- block_input: bfloat16 [2, 8192, 3072], P('cfg', ('ctx', 'tp')), may hold values from -120 to 120
- cached_out: bfloat16 [2, 8192, 3072], P('cfg', ('ctx', 'tp')), may hold values from -120 to 120
- replay_mask: int32 [2, 8192], P('cfg', 'ctx'), may hold values from 0 to 1, as said below
- branch_gate: float32 [2, 3072], P('cfg'), may hold values from 1 to 4
- attn_weight: bfloat16 [3072, 3072], P('tp'), may hold values from -0.109375 to 0.109375
- final_shift: float32 [2, 3072], P('cfg'), may hold values from -4 to 4
- final_scale: float32 [2, 3072], P('cfg'), may hold values from -2 to 2
- patch_weight: bfloat16 [3072, 64], replicated, may hold values from -0.109375 to 0.109375
Outputs:
- block_out: bfloat16 [2, 8192, 3072], P('cfg', ('ctx', 'tp'))
- velocity: float32 [8192, 64], P(('ctx', 'tp'), 'cfg')
Inputs may be any that keep to these rules, and one draw needn't show every extreme that they name: `replay_mask`: in each branch, at most 128 of the 256 rows of one index of ctx have a 0, and some index of ctx has exactly 128.
All inputs are finite; a program needn't handle non-finite values.
Results may differ from a plain program's by a relative error of at most 0.0097.
Values may be sent and summed in bfloat16 or wider, within the bound.
A program may use at most 128 MiB of HBM per device.

v0:
```python
import jax
import jax.numpy as jnp
from jax import lax
from jax.sharding import PartitionSpec as P

guidance_scale = 3.0


def sent_together(arrays, axis, dim, along):
    widths = [a.shape[along] for a in arrays]
    both = jnp.concatenate(arrays, axis=along)
    filled = lax.all_gather(both, axis, axis=dim, tiled=True)
    return tuple(jnp.split(filled, [sum(widths[:k]) for k in range(1, len(widths))], axis=along))


def norm_heads(values, gain):
    width = values.shape[-1]
    depth = gain.shape[0]
    lifted = values.astype(jnp.float32).reshape(values.shape[:-1] + (width // depth, depth))
    mean_square = jnp.mean(lifted * lifted, axis=-1, keepdims=True)
    scaled = lifted * lax.rsqrt(mean_square + 1e-06) * gain
    return scaled.reshape(values.shape).astype(jnp.bfloat16)


def absorb(state, keys_part, values_part, query_heads):
    heads = query_heads.shape[0]
    depth = query_heads.shape[2]
    length = keys_part.shape[0]
    block = 512
    key_blocks = keys_part.reshape(length // block, block, heads, depth)
    value_blocks = values_part.reshape(length // block, block, heads, depth)
    scale = depth ** (-0.5)

    def update(carried, blocks):
        summed, biggest, totals = carried
        keys_here, values_here = blocks
        scores = (
            jnp.einsum("hqd,khd->hqk", query_heads, keys_here, preferred_element_type=jnp.float32)
            * scale
        )
        newest = jnp.maximum(biggest, jnp.max(scores, axis=-1))
        factor = jnp.exp(biggest - newest)
        weights = jnp.exp(scores - newest[..., None])
        totals = totals * factor + jnp.sum(weights, axis=-1)
        added = jnp.einsum(
            "hqk,khd->hqd",
            weights.astype(jnp.bfloat16),
            values_here,
            preferred_element_type=jnp.float32,
        )
        summed = summed * factor[..., None] + added
        return ((summed, newest, totals), None)

    state, unused = lax.scan(update, state, (key_blocks, value_blocks))
    return state


def shards(
    query_proj,
    key_proj,
    value_proj,
    query_gain,
    key_gain,
    block_input,
    cached_out,
    replay_mask,
    branch_gate,
    attn_weight,
    final_shift,
    final_scale,
    patch_weight,
):
    count = query_proj.shape[1]
    width = query_proj.shape[2]
    depth = query_gain.shape[0]
    heads = width // depth
    live_count = count // 2
    share = count // lax.axis_size("tp")
    queries = norm_heads(query_proj[0], query_gain)
    keys_normed = norm_heads(key_proj[0], key_gain)
    values_local = value_proj[0]
    mask_local = replay_mask[0]
    selected = jnp.argsort(mask_local, stable=True)[:live_count]
    picked = queries[selected]
    picked_count = picked.shape[0]
    query_heads = picked.reshape(picked_count, heads, depth).transpose(1, 0, 2)
    start_state = (
        jnp.zeros((heads, picked_count, depth), jnp.float32),
        jnp.full((heads, picked_count), -1e30, jnp.float32),
        jnp.zeros((heads, picked_count), jnp.float32),
    )
    piece = sent_together((keys_normed, values_local), "ctx", 0, 1)
    state = absorb(start_state, piece[0], piece[1], query_heads)
    summed, biggest, totals = state
    attended_picked = (
        (summed / totals[..., None])
        .transpose(1, 0, 2)
        .reshape(picked_count, width)
        .astype(jnp.bfloat16)
    )
    attended = jnp.zeros((count, width), jnp.bfloat16).at[selected].set(attended_picked)
    projected = lax.psum_scatter(
        jnp.dot(attended, attn_weight, preferred_element_type=jnp.float32).astype(jnp.bfloat16),
        "tp",
        scatter_dimension=0,
        tiled=True,
    ).astype(jnp.float32)
    mask_rows = lax.dynamic_slice_in_dim(mask_local, lax.axis_index("tp") * share, share, 0)
    mixed = block_input[0].astype(jnp.float32) + branch_gate[0][None, :] * projected
    block_out = jnp.where(mask_rows[:, None] == 1, cached_out[0].astype(jnp.float32), mixed).astype(
        jnp.bfloat16
    )
    lifted = block_out.astype(jnp.float32)
    center = jnp.mean(lifted, axis=-1, keepdims=True)
    spread = jnp.mean((lifted - center) * (lifted - center), axis=-1, keepdims=True)
    normed = (
        (lifted - center) * lax.rsqrt(spread + 1e-06) * (1.0 + final_scale[0][None, :])
        + final_shift[0][None, :]
    ).astype(jnp.bfloat16)
    branch_out = jnp.dot(normed, patch_weight, preferred_element_type=jnp.float32)
    paired = lax.all_to_all(branch_out, "cfg", split_axis=1, concat_axis=0, tiled=True)
    cond_part = paired[:share]
    uncond_part = paired[share:]
    velocity = uncond_part + guidance_scale * (cond_part - uncond_part)
    return (block_out[None], velocity)


def solution(mesh):
    in_specs = (
        P("cfg", "ctx", "tp"),
        P("cfg", "ctx", "tp"),
        P("cfg", "ctx", "tp"),
        P(),
        P(),
        P("cfg", ("ctx", "tp"), None),
        P("cfg", ("ctx", "tp"), None),
        P("cfg", "ctx"),
        P("cfg", None),
        P("tp", None),
        P("cfg", None),
        P("cfg", None),
        P(),
    )
    out_specs = (P("cfg", ("ctx", "tp"), None), P(("ctx", "tp"), "cfg"))
    return jax.shard_map(shards, mesh=mesh, in_specs=in_specs, out_specs=out_specs, check_vma=False)
```

profile of v0, /device:TPU:8, one launch (start us, length us, event | category | flops | bytes accessed | tf_op | source)
XLA Modules:
  0.0 299.3 jit_solution(18116649159860371368)
XLA Ops:
  7.3 1.2 copy.30
  13.3 1.2 copy.33
  14.5 3.2 %sort.17 = (s32[256]{0:T(256)}, s32[256]{0:T(256)S(1)}) sort(s32[256]{0:T(256)S(1)} %bitcast.110, s32[256]{0:T(256)S(1)} %iota.4), dimensions={0}, to_apply=%region_0.0 | sort | flops 2048 | bytes 4096 | tf_op jit(solution)/shard_map/jit(argsort)/sort | solution.py:83
  19.4 131.4 %all-gather.2.cloned.1.call-done = bf16[8192,768]{0,1:T(8,128)(2,1)} async-done(((bf16[256,768]{0,1:T(8,128)(2,1)}), bf16[8192,768]{0,1:T(8,128)(2,1)}) %all-gather.2.cloned.1.call-update) | async-done | bytes 12582928 | tf_op jit(solution)/shard_map/all_gather | solution.py:12
  150.8 8.2 %fusion.39 = (bf16[8192,384]{0,1:T(8,128)(2,1)}, bf16[8192,384]{0,1:T(8,128)(2,1)S(1)}) fusion(bf16[8192,768]{0,1:T(8,128)(2,1)} %all-gather.2.cloned.1.call-done), kind=kLoop, calls=%fused_computation.67 | loop fusion | bytes 25165824 | tf_op jit(solution)/shard_map/split | solution.py:13
  159.0 5.6 %copy.42 = bf16[48,8,16,512]{3,2,1,0:T(8,128)(2,1)} copy(bf16[48,8,16,512]{3,1,2,0:T(8,128)(2,1)S(1)} %bitcast.99) | data formatting | bytes 12582912
  164.6 9.1 %copy.35 = bf16[16,512,3,128]{3,1,2,0:T(8,128)(2,1)} copy(bf16[16,512,3,128]{1,0,3,2:T(8,128)(2,1)} %bitcast.96) | data formatting | bytes 12582912
  173.7 8.3 %copy.43 = bf16[48,8,16,512]{3,2,1,0:T(8,128)(2,1)} copy(bf16[48,8,16,512]{3,1,2,0:T(8,128)(2,1)} %bitcast.98) | data formatting | bytes 12582912
  182.0 9.2 %copy.37 = bf16[16,512,3,128]{3,1,2,0:T(8,128)(2,1)} copy(bf16[16,512,3,128]{1,0,3,2:T(8,128)(2,1)} %bitcast.97) | data formatting | bytes 12582912
  191.2 45.7 %while.15 = (s32[]{:T(128)}, f32[3,128,128]{2,1,0:T(8,128)S(1)}, f32[3,128]{1,0:T(4,128)S(1)}, f32[3,128]{1,0:T(4,128)S(1)}, bf16[16,512,3,128]{3,1,2,0:T(8,128)...) while((s32[]{:T(128)}, f32[3,128,128]{2,1,0:T(8,128)S(1)}, ...), condition=%wide.region_6.7_spmd.clone, body=%wide.region_3.6_spmd.clone.sunk | while | flops 101992320 | bytes 3662953 | solution.py:54
  191.2 1.3 fusion.53
  192.6 1.4 convolution_add_fusion.2
  194.0 1.3 fusion.53
  195.5 1.4 convolution_add_fusion.2
  196.9 1.3 fusion.53
  198.3 1.4 convolution_add_fusion.2
  199.7 1.3 fusion.53
  201.2 1.4 convolution_add_fusion.2
  202.6 1.3 fusion.53
  204.1 1.4 convolution_add_fusion.2
  205.5 1.3 fusion.53
  206.9 1.4 convolution_add_fusion.2
  208.3 1.3 fusion.53
  209.8 1.4 convolution_add_fusion.2
  211.2 1.3 fusion.53
  212.6 1.4 convolution_add_fusion.2
  214.0 1.3 fusion.53
  215.5 1.4 convolution_add_fusion.2
  216.9 1.3 fusion.53
  218.3 1.4 convolution_add_fusion.2
  219.7 1.3 fusion.53
  221.2 1.4 convolution_add_fusion.2
  222.6 1.3 fusion.53
  224.0 1.4 convolution_add_fusion.2
  225.4 1.3 fusion.53
  226.9 1.4 convolution_add_fusion.2
  228.3 1.3 fusion.53
  229.7 1.4 convolution_add_fusion.2
  231.2 1.3 fusion.53
  232.6 1.4 convolution_add_fusion.2
  234.0 1.3 fusion.53
  235.5 1.4 convolution_add_fusion.2
  237.2 1.2 scatter_custom_fusion
  238.5 2.1 convolution_convert_fusion
  240.7 40.6 %reduce-scatter.2.cloned.1.call-done = bf16[32,3072]{1,0:T(8,128)(2,1)} async-done(((bf16[256,3072]{1,0:T(8,128)(2,1)}), bf16[32,3072]{1,0:T(8,128)(2,1)}) %reduce-scatter.2.cloned.1.call-update) | async-done | bytes 196624 | tf_op jit(solution)/shard_map/reduce_scatter | solution.py:102
  281.3 1.1 convert_reduce_fusion
  282.7 1.3 fusion.26
  284.2 6.3 %all_to_all.16 = f32[2,1,1024]{2,1,0:T(1,128)S(1)} all-to-all(f32[2,1,1024]{2,1,0:T(1,128)S(1)} %reshape.115), channel_id=1, replica_groups=mesh['cfg'=2,'ctx'=32,'tp'=8] {'cfg'}, dimensions={0} | all-to-all | bytes 16384 | tf_op jit(solution)/shard_map/all_to_all | solution.py:121
  (129 shorter events, 11.7 us)
Async XLA Ops:
  7.2 231.3 %copy-start = (bf16[384,3072]{1,0:T(8,128)(2,1)S(1)}, bf16[384,3072]{1,0:T(8,128)(2,1)}, u32[]{:S(2)}) copy-start(bf16[384,3072]{1,0:T(8,128)(2,1)} %param.24) | copy-start | bytes 7077892
  7.2 11.0 %copy-start.2 = (bf16[1,256,384]{2,1,0:T(8,128)(2,1)S(1)}, bf16[1,256,384]{2,1,0:T(8,128)(2,1)}, u32[]{:S(2)}) copy-start(bf16[1,256,384]{2,1,0:T(8,128)(2,1)} %param.15) | copy-start | bytes 589828
  7.2 7.3 %copy-start.7 = (s32[1,256]{1,0:T(1,128)S(1)}, s32[1,256]{1,0:T(1,128)}, u32[]{:S(2)}) copy-start(s32[1,256]{1,0:T(1,128)} %param.22) | copy-start | bytes 3076
  7.2 11.0 %copy-start.8 = (f32[128]{0:T(128)S(1)}, f32[128]{0:T(128)}, u32[]{:S(2)}) copy-start(f32[128]{0:T(128)} %param.18) | copy-start | bytes 1540
  7.2 143.6 %all-gather.2.cloned.1.call-start = ((), (), s32[]{:S(2)}) async-start(), calls=%async_computation.2 | async-start | bytes 12976128 | tf_op jit(solution)/shard_map/all_gather | solution.py:12
  11.2 270.1 %reduce-scatter.2.cloned.1.call-start = ((), (), s32[]{:S(2)}) async-start(), calls=%async_computation.3 | async-start | bytes 1769472 | tf_op jit(solution)/shard_map/reduce_scatter | solution.py:102
  17.7 0.5 copy-start.9
  236.9 3.8 %copy-start.5 = (f32[1,3072]{1,0:T(1,128)S(1)}, f32[1,3072]{1,0:T(1,128)}, u32[]{:S(2)}) copy-start(f32[1,3072]{1,0:T(1,128)} %param.26) | copy-start | bytes 36868
  236.9 44.5 %copy-start.3 = (bf16[1,32,3072]{2,1,0:T(8,128)(2,1)S(1)}, bf16[1,32,3072]{2,1,0:T(8,128)(2,1)}, u32[]{:S(2)}) copy-start(bf16[1,32,3072]{2,1,0:T(8,128)(2,1)} %param.20) | copy-start | bytes 589828
  236.9 44.4 %copy-start.4 = (bf16[1,32,3072]{2,1,0:T(8,128)(2,1)S(1)}, bf16[1,32,3072]{2,1,0:T(8,128)(2,1)}, u32[]{:S(2)}) copy-start(bf16[1,32,3072]{2,1,0:T(8,128)(2,1)} %param.21) | copy-start | bytes 589828
  236.9 44.4 %copy-start.6 = (f32[1,3072]{1,0:T(1,128)S(1)}, f32[1,3072]{1,0:T(1,128)}, u32[]{:S(2)}) copy-start(f32[1,3072]{1,0:T(1,128)} %param.23) | copy-start | bytes 36868
  236.9 45.8 %copy-start.10 = (f32[1,3072]{1,0:T(1,128)S(1)}, f32[1,3072]{1,0:T(1,128)}, u32[]{:S(2)}) copy-start(f32[1,3072]{1,0:T(1,128)} %param.25) | copy-start | bytes 36868
  282.5 10.0 %copy-start.1 = (bf16[32,3072]{1,0:T(8,128)(2,1)}, bf16[32,3072]{1,0:T(8,128)(2,1)S(1)}, u32[]{:S(2)}) copy-start(bf16[32,3072]{1,0:T(8,128)(2,1)S(1)} %get-tuple-element.99) | copy-start | bytes 589828
Sparse Core Ops, SparseCore 0:
  11.4 139.4 all-gather.1
  240.7 40.5 reduce-scatter.1
where the time goes:
time: 301 us; the launch traced here: 299 us
  waiting for transfers between devices  172 us (57%)
  local copies, waits for them, and re-layouts  49.4 us (16%)
  matrix products  45.9 us (15%)
  between operations  14.3 us (5%)
  other arithmetic  10.4 us (3%)
  blocking collectives  6.35 us (2%)
    all_gather x1, waiting for transfers between devices, sent_together(): filled = lax.all_gather(both, axis, axis=dim, tiled=True)  131 us
    reduce_scatter x1, waiting for transfers between devices, shards(): lax.psum_scatter(jnp.dot(attended, attn_weight, preferred_element_type=jn...  40.6 us
    unnamed x31, local copies, waits for them, and re-layouts  35.3 us
    dot_general x16, matrix products, update(): jnp.einsum('hqk,khd->hqd', weights.astype(jnp.bfloat16), values_here, pre...  22 us
    dot_general x16, matrix products, update(): jnp.einsum('hqd,khd->hqk', query_heads, keys_here, preferred_element_type...  20.5 us
    split x1, local copies, waits for them, and re-layouts, sent_together(): jnp.split(filled, [sum(widths[:k]) for k in range(1, len(widths))], axis=...  8.21 us
    all_to_all x1, blocking collectives, shards(): lax.all_to_all(branch_out, 'cfg', split_axis=1, concat_axis=0, tiled=True)  6.35 us
  transfers between devices with their start and end apart: 2, of which 2 were waited for; matrix products, arithmetic and copies ran while one was open for 3% of the time, Pallas kernels for 0%

commit v1 on v0

--- a/solution.py
+++ b/solution.py
@@ -118,7 +118,15 @@
         + final_shift[0][None, :]
     ).astype(jnp.bfloat16)
     branch_out = jnp.dot(normed, patch_weight, preferred_element_type=jnp.float32)
-    paired = lax.all_to_all(branch_out, "cfg", split_axis=1, concat_axis=0, tiled=True)
+
+    def draft_corner(payload, along_axis):
+        front = lax.all_to_all(
+            jnp.stack(jnp.split(payload, lax.axis_size(along_axis), 1), 0), along_axis, 0, 0
+        )
+        v1 = jnp.concatenate(front, 0)
+        return v1
+
+    paired = draft_corner(branch_out, "cfg")
     cond_part = paired[:share]
     uncond_part = paired[share:]
     velocity = uncond_part + guidance_scale * (cond_part - uncond_part)

time: 301 us -> 301 us (level)
  no operation moved by 1% of the time
where the time goes in v1:
time: 301 us; the launch traced here: 299 us
  waiting for transfers between devices  172 us (57%)
  local copies, waits for them, and re-layouts  49.4 us (16%)
  matrix products  45.9 us (15%)
  between operations  14.3 us (5%)
  other arithmetic  10.5 us (3%)
  blocking collectives  6.35 us (2%)
    all_gather x1, waiting for transfers between devices, sent_together(): filled = lax.all_gather(both, axis, axis=dim, tiled=True)  131 us
    reduce_scatter x1, waiting for transfers between devices, shards(): lax.psum_scatter(jnp.dot(attended, attn_weight, preferred_element_type=jn...  40.6 us
    unnamed x31, local copies, waits for them, and re-layouts  35.3 us
    dot_general x16, matrix products, update(): jnp.einsum('hqk,khd->hqd', weights.astype(jnp.bfloat16), values_here, pre...  22 us
    dot_general x16, matrix products, update(): jnp.einsum('hqd,khd->hqk', query_heads, keys_here, preferred_element_type...  20.5 us
    split x1, local copies, waits for them, and re-layouts, sent_together(): jnp.split(filled, [sum(widths[:k]) for k in range(1, len(widths))], axis=...  8.21 us
    all_to_all x1, blocking collectives, draft_corner(): lax.all_to_all(jnp.stack(jnp.split(payload, lax.axis_size(along_axis), 1)...  6.35 us
  transfers between devices with their start and end apart: 2, of which 2 were waited for; matrix products, arithmetic and copies ran while one was open for 3% of the time, Pallas kernels for 0%

profile of v1, /device:TPU:8, one launch (start us, length us, event | category | flops | bytes accessed | tf_op | source)
XLA Modules:
  0.0 299.3 jit_solution(3516769743607256806)
XLA Ops:
  7.3 1.2 copy.28
  13.3 1.2 copy.31
  14.5 3.2 %sort.17 = (s32[256]{0:T(256)}, s32[256]{0:T(256)S(1)}) sort(s32[256]{0:T(256)S(1)} %bitcast.106, s32[256]{0:T(256)S(1)} %iota.4), dimensions={0}, to_apply=%region_0.0 | sort | flops 2048 | bytes 4096 | tf_op jit(solution)/shard_map/jit(argsort)/sort | solution.py:83
  19.4 131.4 %all-gather.2.cloned.1.call-done = bf16[8192,768]{0,1:T(8,128)(2,1)} async-done(((bf16[256,768]{0,1:T(8,128)(2,1)}), bf16[8192,768]{0,1:T(8,128)(2,1)}) %all-gather.2.cloned.1.call-update) | async-done | bytes 12582928 | tf_op jit(solution)/shard_map/all_gather | solution.py:12
  150.8 8.2 %fusion.39 = (bf16[8192,384]{0,1:T(8,128)(2,1)}, bf16[8192,384]{0,1:T(8,128)(2,1)S(1)}) fusion(bf16[8192,768]{0,1:T(8,128)(2,1)} %all-gather.2.cloned.1.call-done), kind=kLoop, calls=%fused_computation.70 | loop fusion | bytes 25165824 | tf_op jit(solution)/shard_map/split | solution.py:13
  159.0 5.6 %copy.39 = bf16[48,8,16,512]{3,2,1,0:T(8,128)(2,1)} copy(bf16[48,8,16,512]{3,1,2,0:T(8,128)(2,1)S(1)} %bitcast.96) | data formatting | bytes 12582912
  164.6 9.1 %copy.33 = bf16[16,512,3,128]{3,1,2,0:T(8,128)(2,1)} copy(bf16[16,512,3,128]{1,0,3,2:T(8,128)(2,1)} %bitcast.93) | data formatting | bytes 12582912
  173.7 8.3 %copy.40 = bf16[48,8,16,512]{3,2,1,0:T(8,128)(2,1)} copy(bf16[48,8,16,512]{3,1,2,0:T(8,128)(2,1)} %bitcast.95) | data formatting | bytes 12582912
  182.0 9.2 %copy.35 = bf16[16,512,3,128]{3,1,2,0:T(8,128)(2,1)} copy(bf16[16,512,3,128]{1,0,3,2:T(8,128)(2,1)} %bitcast.94) | data formatting | bytes 12582912
  191.2 45.7 %while.15 = (s32[]{:T(128)}, f32[3,128,128]{2,1,0:T(8,128)S(1)}, f32[3,128]{1,0:T(4,128)S(1)}, f32[3,128]{1,0:T(4,128)S(1)}, bf16[16,512,3,128]{3,1,2,0:T(8,128)...) while((s32[]{:T(128)}, f32[3,128,128]{2,1,0:T(8,128)S(1)}, ...), condition=%wide.region_6.7_spmd.clone, body=%wide.region_3.6_spmd.clone.sunk | while | flops 101992320 | bytes 3662953 | solution.py:54
  191.2 1.3 fusion.53
  192.6 1.4 convolution_add_fusion.2
  194.0 1.3 fusion.53
  195.5 1.4 convolution_add_fusion.2
  196.9 1.3 fusion.53
  198.3 1.4 convolution_add_fusion.2
  199.7 1.3 fusion.53
  201.2 1.4 convolution_add_fusion.2
  202.6 1.3 fusion.53
  204.1 1.4 convolution_add_fusion.2
  205.5 1.3 fusion.53
  206.9 1.4 convolution_add_fusion.2
  208.3 1.3 fusion.53
  209.8 1.4 convolution_add_fusion.2
  211.2 1.3 fusion.53
  212.6 1.4 convolution_add_fusion.2
  214.0 1.3 fusion.53
  215.5 1.4 convolution_add_fusion.2
  216.9 1.3 fusion.53
  218.3 1.4 convolution_add_fusion.2
  219.7 1.3 fusion.53
  221.2 1.4 convolution_add_fusion.2
  222.6 1.3 fusion.53
  224.0 1.4 convolution_add_fusion.2
  225.4 1.3 fusion.53
  226.9 1.4 convolution_add_fusion.2
  228.3 1.3 fusion.53
  229.7 1.4 convolution_add_fusion.2
  231.2 1.3 fusion.53
  232.6 1.4 convolution_add_fusion.2
  234.0 1.3 fusion.53
  235.5 1.4 convolution_add_fusion.2
  237.2 1.2 scatter_custom_fusion
  238.5 2.1 convolution_convert_fusion
  240.7 40.6 %reduce-scatter.2.cloned.1.call-done = bf16[32,3072]{1,0:T(8,128)(2,1)} async-done(((bf16[256,3072]{1,0:T(8,128)(2,1)}), bf16[32,3072]{1,0:T(8,128)(2,1)}) %reduce-scatter.2.cloned.1.call-update) | async-done | bytes 196624 | tf_op jit(solution)/shard_map/reduce_scatter | solution.py:102
  281.3 1.1 convert_reduce_fusion
  282.7 1.3 fusion.26
  284.2 6.3 %all_to_all.5 = f32[2,1,1024]{2,1,0:T(1,128)S(1)} all-to-all(f32[2,1,1024]{2,1,0:T(1,128)S(1)} %reshape.113), channel_id=1, replica_groups=mesh['cfg'=2,'ctx'=32,'tp'=8] {'cfg'}, dimensions={0} | all-to-all | bytes 16384 | tf_op jit(solution)/shard_map/all_to_all | solution.py:123
  (128 shorter events, 11.7 us)
Async XLA Ops:
  7.2 231.3 %copy-start = (bf16[384,3072]{1,0:T(8,128)(2,1)S(1)}, bf16[384,3072]{1,0:T(8,128)(2,1)}, u32[]{:S(2)}) copy-start(bf16[384,3072]{1,0:T(8,128)(2,1)} %param.24) | copy-start | bytes 7077892
  7.2 11.0 %copy-start.2 = (bf16[1,256,384]{2,1,0:T(8,128)(2,1)S(1)}, bf16[1,256,384]{2,1,0:T(8,128)(2,1)}, u32[]{:S(2)}) copy-start(bf16[1,256,384]{2,1,0:T(8,128)(2,1)} %param.15) | copy-start | bytes 589828
  7.2 7.3 %copy-start.7 = (s32[1,256]{1,0:T(1,128)S(1)}, s32[1,256]{1,0:T(1,128)}, u32[]{:S(2)}) copy-start(s32[1,256]{1,0:T(1,128)} %param.22) | copy-start | bytes 3076
  7.2 11.0 %copy-start.8 = (f32[128]{0:T(128)S(1)}, f32[128]{0:T(128)}, u32[]{:S(2)}) copy-start(f32[128]{0:T(128)} %param.18) | copy-start | bytes 1540
  7.2 143.6 %all-gather.2.cloned.1.call-start = ((), (), s32[]{:S(2)}) async-start(), calls=%async_computation.2 | async-start | bytes 12976128 | tf_op jit(solution)/shard_map/all_gather | solution.py:12
  11.2 270.1 %reduce-scatter.2.cloned.1.call-start = ((), (), s32[]{:S(2)}) async-start(), calls=%async_computation.3 | async-start | bytes 1769472 | tf_op jit(solution)/shard_map/reduce_scatter | solution.py:102
  17.7 0.5 copy-start.9
  236.9 3.8 %copy-start.5 = (f32[1,3072]{1,0:T(1,128)S(1)}, f32[1,3072]{1,0:T(1,128)}, u32[]{:S(2)}) copy-start(f32[1,3072]{1,0:T(1,128)} %param.26) | copy-start | bytes 36868
  236.9 44.5 %copy-start.3 = (bf16[1,32,3072]{2,1,0:T(8,128)(2,1)S(1)}, bf16[1,32,3072]{2,1,0:T(8,128)(2,1)}, u32[]{:S(2)}) copy-start(bf16[1,32,3072]{2,1,0:T(8,128)(2,1)} %param.20) | copy-start | bytes 589828
  236.9 44.4 %copy-start.4 = (bf16[1,32,3072]{2,1,0:T(8,128)(2,1)S(1)}, bf16[1,32,3072]{2,1,0:T(8,128)(2,1)}, u32[]{:S(2)}) copy-start(bf16[1,32,3072]{2,1,0:T(8,128)(2,1)} %param.21) | copy-start | bytes 589828
  236.9 44.4 %copy-start.6 = (f32[1,3072]{1,0:T(1,128)S(1)}, f32[1,3072]{1,0:T(1,128)}, u32[]{:S(2)}) copy-start(f32[1,3072]{1,0:T(1,128)} %param.23) | copy-start | bytes 36868
  236.9 45.8 %copy-start.10 = (f32[1,3072]{1,0:T(1,128)S(1)}, f32[1,3072]{1,0:T(1,128)}, u32[]{:S(2)}) copy-start(f32[1,3072]{1,0:T(1,128)} %param.25) | copy-start | bytes 36868
  282.5 10.0 %copy-start.1 = (bf16[32,3072]{1,0:T(8,128)(2,1)}, bf16[32,3072]{1,0:T(8,128)(2,1)S(1)}, u32[]{:S(2)}) copy-start(bf16[32,3072]{1,0:T(8,128)(2,1)S(1)} %get-tuple-element.99) | copy-start | bytes 589828
Sparse Core Ops, SparseCore 0:
  11.4 139.4 all-gather.1
  240.7 40.5 reduce-scatter.1
